TPU v7x, 32 devices: a whole 2x2x4 slice. The times are simulated.
32 devices in a mesh: dp: 8 (over y, x, core), fsdp: 4 (over z).
Axes of the slice: x: 2, y: 2, z: 4, core: 2. Of those that a mesh axis runs over, the one named last changes fastest.
Arguments:
- grads: float32 [32, 96, 128], P(('dp', 'fsdp')), may hold values from -0.6 to 0.6
- last_peak: float32 [96], replicated, may hold values from 0.05 to 0.8
- master: float32 [96, 128], P(('dp', 'fsdp')), may hold values from -6 to 6
- moment1: float32 [96, 128], P(('dp', 'fsdp')), may hold values from -6 to 6
- moment2: float32 [96, 128], P(('dp', 'fsdp')), may hold values from 0.25 to 8
Outputs:
- new_master: float32 [96, 128], P(('dp', 'fsdp'))
- new_moment1: float32 [96, 128], P(('dp', 'fsdp'))
- new_moment2: float32 [96, 128], P(('dp', 'fsdp'))
- weights: bfloat16 [96, 128], replicated
- block_peak: float32 [96], replicated
All inputs are finite; a program needn't handle non-finite values.
Results may differ from a plain program's by a relative error of at most 0.0035.
Values may be sent and summed in bfloat16 or wider, within the bound.
No kernel may reach another device: no remote copies, remote signals or barrier semaphores. Data moves between devices by JAX's collectives and lax.ppermute only.
A program may use at most 64 MiB of HBM per device.

v0:
```python
import jax
import jax.numpy as jnp
from jax import lax
from jax.sharding import PartitionSpec as P

STEP_COUNT = 10


code_limit = 448.0
peak_floor = 0.05
beta_one = 0.9
beta_two = 0.95
learn_rate = 0.05
decay_rate = 0.1
epsilon = 1e-08


def quantize(rows, inverse):
    codes = jnp.clip(rows * inverse[:, None], -code_limit, code_limit).astype(jnp.bfloat16)
    return lax.optimization_barrier(codes).astype(jnp.float32)


def adamw(gradient, master, moment1, moment2):
    first = beta_one * moment1 + (1.0 - beta_one) * gradient
    second = beta_two * moment2 + (1.0 - beta_two) * gradient * gradient
    corrected_one = first / (1.0 - beta_one**STEP_COUNT)
    corrected_two = second / (1.0 - beta_two**STEP_COUNT)
    updated = master - learn_rate * (
        corrected_one / (jnp.sqrt(corrected_two) + epsilon) + decay_rate * master
    )
    return (updated, first, second)


def body(grads, last_peak, master, moment1, moment2):
    local = grads[0]
    peak = lax.pmax(jnp.max(jnp.abs(local), axis=1), ("dp", "fsdp"))
    floored = jnp.maximum(last_peak, peak_floor)
    inverse = code_limit / floored
    scale = floored / code_limit
    owned = master.shape[0]
    first_row = lax.axis_index(("dp", "fsdp")) * owned
    summed = lax.psum_scatter(
        quantize(local, inverse), ("dp", "fsdp"), scatter_dimension=0, tiled=True
    )
    own_scale = lax.dynamic_slice_in_dim(scale, first_row, owned, 0)
    gradient = summed * own_scale[:, None]
    updated, first, second = adamw(gradient, master, moment1, moment2)
    rounded = updated.astype(jnp.bfloat16)
    grouped_rows = lax.all_gather(rounded, "fsdp", axis=0, tiled=True)
    weights = lax.all_gather(grouped_rows, "dp", axis=0, tiled=True)
    return (updated, first, second, weights, peak)


def solution(mesh):
    placed = (
        P(("dp", "fsdp"), None, None),
        P(),
        P(("dp", "fsdp"), None),
        P(("dp", "fsdp"), None),
        P(("dp", "fsdp"), None),
    )
    return jax.shard_map(
        body,
        mesh=mesh,
        in_specs=placed,
        out_specs=(
            P(("dp", "fsdp"), None),
            P(("dp", "fsdp"), None),
            P(("dp", "fsdp"), None),
            P(),
            P(),
        ),
        check_vma=False,
    )
```

profile of v0, /device:TPU:0, one launch (start us, length us, event | category | flops | bytes accessed | tf_op | source)
XLA Modules:
  0.0 103.8 jit_solution(240758746087156561)
XLA Ops:
  0.6 0.0 copy-start.3
  0.6 0.6 copy-done.3
  1.3 0.1 dynamic_slice.3
  1.4 1.0 fusion.2
  2.4 42.3 %all-reduce = f32[96,128]{1,0:T(8,128)S(1)} all-reduce(bf16[96,128]{1,0:T(8,128)(2,1)S(1)} %get-tuple-element.10), channel_id=2, replica_groups=mesh['dp'=8,'fsdp'=4] {'dp','fsdp'}, use_global_device_ids=true, to_apply=%region_0.0.clone | all-reduce | flops 12288 | bytes 73728
  44.7 0.0 copy-start.2
  44.7 0.0 copy-start
  44.7 0.0 copy-start.1
  44.7 0.6 copy-done.2
  45.4 0.0 copy-done
  45.4 0.0 copy-done.1
  45.4 0.7 convert_bitcast_fusion
  46.1 9.8 %all-gather = bf16[4,3,128]{2,1,0:T(4,128)(2,1)S(1)} all-gather(bf16[1,3,128]{2,1,0:T(4,128)(2,1)S(1)} %get-tuple-element.5), channel_id=1, replica_groups=mesh['dp'=8,'fsdp'=4] {'fsdp'}, dimensions={0}, use_global_device_ids=true | all-gather | bytes 3840 | tf_op jit(solution)/shard_map/all_gather | solution.py:49
  55.9 9.9 %all-gather.1 = bf16[8,12,128]{2,1,0:T(8,128)(2,1)S(1)} all-gather(bf16[1,12,128]{2,1,0:T(8,128)(2,1)S(1)} %reshape.14), channel_id=1, replica_groups=mesh['dp'=8,'fsdp'=4] {'dp'}, dimensions={0}, use_global_device_ids=true | all-gather | bytes 27648 | tf_op jit(solution)/shard_map/all_gather | solution.py:50
  65.7 0.6 reshape.15
  66.3 37.4 %pmax.7 = f32[96]{0:T(128)} all-reduce(f32[96]{0:T(128)S(1)} %get-tuple-element.9), channel_id=1, replica_groups=mesh['dp'=8,'fsdp'=4] {'dp','fsdp'}, use_global_device_ids=true, to_apply=%region_2.3 | all-reduce | flops 96 | bytes 768 | tf_op jit(solution)/shard_map/pmax | solution.py:36
  (2 shorter events, 0.0 us)
Async XLA Ops:
  0.6 0.7 copy-start.3
  44.7 0.7 copy-start.2
  44.7 0.7 copy-start
  44.7 0.7 copy-start.1
where the time goes:
time: 104 us
  blocking collectives  99.4 us (96%)
  local copies, waits for them, and re-layouts  2.05 us (2%)
  other arithmetic  1.66 us (2%)
    unnamed x1, blocking collectives  42.3 us
    pmax x1, blocking collectives, body(): peak = lax.pmax(jnp.max(jnp.abs(local), axis=1), ('dp', 'fsdp'))  37.4 us
    all_gather x1, blocking collectives, body(): weights = lax.all_gather(grouped_rows, 'dp', axis=0, tiled=True)  9.86 us
    all_gather x1, blocking collectives, body(): grouped_rows = lax.all_gather(rounded, 'fsdp', axis=0, tiled=True)  9.76 us

commit v1 on v0

v1 whole, which is shorter than its diff:
```python
import jax
import jax.numpy as jnp
from jax import lax
from jax.sharding import PartitionSpec as P

STEP_COUNT = 10


code_limit = 448.0
peak_floor = 0.05
beta_one = 0.9
beta_two = 0.95
learn_rate = 0.05
decay_rate = 0.1
epsilon = 1e-08

axes = ("dp", "fsdp")


def adamw(gradient, master, moment1, moment2):
    first = beta_one * moment1 + (1.0 - beta_one) * gradient
    second = beta_two * moment2 + (1.0 - beta_two) * gradient * gradient
    corrected_one = first / (1.0 - beta_one**STEP_COUNT)
    corrected_two = second / (1.0 - beta_two**STEP_COUNT)
    updated = master - learn_rate * (
        corrected_one / (jnp.sqrt(corrected_two) + epsilon) + decay_rate * master
    )
    return (updated, first, second)


def pieces_of(values):
    high = lax.reduce_precision(values, 8, 7)
    rest = values - high
    middle = lax.reduce_precision(rest, 8, 7)
    return (high, middle, rest - middle)


def packed_row(values, width):
    flat = jnp.concatenate(pieces_of(values), axis=-1)
    rows = -(-flat.shape[-1] // width)
    pad = [(0, 0)] * (flat.ndim - 1) + [(0, rows * width - flat.shape[-1])]
    return jnp.pad(flat, pad).reshape(*flat.shape[:-1], rows, width).astype(jnp.bfloat16)


def unpacked_row(rows, count):
    flat = rows.reshape(*rows.shape[:-2], -1).astype(jnp.float32)
    return (flat[..., :count] + flat[..., count : 2 * count]) + flat[..., 2 * count : 3 * count]


def body(grads, last_peak, master, moment1, moment2):
    owned, width = master.shape
    devices = grads.shape[1] // owned
    local = grads.reshape(devices, owned, width)
    floored = jnp.maximum(last_peak, peak_floor)
    inverse = (code_limit / floored).reshape(devices, owned, 1)
    scale = floored / code_limit
    codes = jnp.clip(local * inverse, -code_limit, code_limit).astype(jnp.bfloat16)
    local_peak = jnp.max(jnp.abs(local), axis=2)
    sent = jnp.concatenate([codes, packed_row(local_peak, width)], axis=1)
    got = lax.all_to_all(sent, axes, 0, 0, tiled=True)
    summed = jnp.sum(got[:, :owned].astype(jnp.float32), axis=0)
    own_peak = jnp.max(unpacked_row(got[:, owned:], owned), axis=0)
    own_scale = lax.dynamic_slice_in_dim(scale, lax.axis_index(axes) * owned, owned, 0)
    gradient = summed * own_scale[:, None]
    updated, first, second = adamw(gradient, master, moment1, moment2)
    mine = jnp.concatenate([updated.astype(jnp.bfloat16), packed_row(own_peak, width)], axis=0)
    everyone = jnp.broadcast_to(mine[None], (devices, *mine.shape))
    spread = lax.all_to_all(everyone, axes, 0, 0, tiled=True)
    weights = spread[:, :owned].reshape(devices * owned, width)
    peak = unpacked_row(spread[:, owned:], owned).reshape(devices * owned)
    return (updated, first, second, weights, peak)


def solution(mesh):
    rows = P(axes, None)
    return jax.shard_map(
        body,
        mesh=mesh,
        in_specs=(P(axes, None, None), P(), rows, rows, rows),
        out_specs=(rows, rows, rows, P(), P()),
        check_vma=False,
    )
```

time: 104 us -> 30.3 us (0.29)
  blocking collectives: 99.4 us -> 8.99 us
  starting transfers between devices: 0 us -> 7.33 us
  waiting for transfers between devices: 0 us -> 7.22 us
  other arithmetic: 1.66 us -> 2.76 us
    unnamed x1 -> x0, blocking collectives: 42.3 us -> none
    pmax x1 -> x0, blocking collectives: 37.4 us -> none  [body(): peak = lax.pmax(jnp.max(jnp.abs(local), axis=1), ('dp', 'fsdp'))]
    all_gather x2 -> x0, blocking collectives: 19.6 us -> none  [the longest x1 9.86 us: body(): weights = lax.all_gather(grouped_rows, 'dp', axis=0, tiled=True)]
    all_to_all x0 -> x1, blocking collectives: none -> 8.99 us  [body(): spread = lax.all_to_all(everyone, axes, 0, 0, tiled=True)]
    all_to_all x0 -> x1, starting transfers between devices: none -> 7.33 us  [body(): got = lax.all_to_all(sent, axes, 0, 0, tiled=True)]
    all_to_all x0 -> x1, waiting for transfers between devices: none -> 7.22 us  [body(): got = lax.all_to_all(sent, axes, 0, 0, tiled=True)]
    reshape x0 -> x3, local copies, waits for them, and re-layouts: none -> 1.28 us  [the longest x1 0.63 us: body(): weights = spread[:, :owned].reshape(devices * owned, width)]
  transfers between devices with their start and end apart: 0 -> 1, of which waited for: 0 -> 1; matrix products, arithmetic and copies ran while one was open for 0% -> 0% of each run, Pallas kernels for 0% -> 0%
where the time goes in v1:
time: 30.3 us; the launch traced here: 30.1 us
  blocking collectives  8.99 us (30%)
  starting transfers between devices  7.33 us (24%)
  waiting for transfers between devices  7.22 us (24%)
  local copies, waits for them, and re-layouts  3.02 us (10%)
  other arithmetic  2.76 us (9%)
  between operations  0.75 us (2%)
    all_to_all x1, blocking collectives, body(): spread = lax.all_to_all(everyone, axes, 0, 0, tiled=True)  8.99 us
    all_to_all x1, starting transfers between devices, body(): got = lax.all_to_all(sent, axes, 0, 0, tiled=True)  7.33 us
    all_to_all x1, waiting for transfers between devices, body(): got = lax.all_to_all(sent, axes, 0, 0, tiled=True)  7.22 us
    unnamed x10, local copies, waits for them, and re-layouts  1.29 us
    reduce_max x1, other arithmetic, body(): local_peak = jnp.max(jnp.abs(local), axis=2)  0.96 us
    convert_element_type x1, other arithmetic, body(): updated.astype(jnp.bfloat16)  0.67 us
    concatenate x1, other arithmetic, body(): sent = jnp.concatenate([codes, packed_row(local_peak, width)], axis=1)  0.65 us
    reshape x1, local copies, waits for them, and re-layouts, body(): weights = spread[:, :owned].reshape(devices * owned, width)  0.63 us
  transfers between devices with their start and end apart: 1, of which 1 were waited for; matrix products, arithmetic and copies ran while one was open for 0% of the time, Pallas kernels for 0%

profile of v1, /device:TPU:0, one launch (start us, length us, event | category | flops | bytes accessed | tf_op | source)
XLA Modules:
  0.0 30.1 jit_solution(6182924393259979205)
XLA Ops:
  0.6 0.0 copy-start
  0.6 1.0 %abs_reduce_fusion = f32[96]{0:T(128)S(1)} fusion(f32[1,96,128]{2,1,0:T(8,128)} %param.5), kind=kLoop, calls=%fused_computation.6 | loop fusion | flops 24480 | bytes 49536 | tf_op jit(solution)/shard_map/reduce_max | solution.py:58
  1.6 0.0 copy-done
  1.6 0.0 copy-start.4
  1.7 0.6 %copy-done.4 = f32[96]{0:T(128)S(1)} copy-done((f32[96]{0:T(128)S(1)}, f32[96]{0:T(128)}, u32[]{:S(2)}) %copy-start.4) | copy-done | bytes 408
  2.3 0.1 reduce_max.21
  2.4 0.1 copy.16
  2.5 0.1 mul.53
  2.6 0.1 copy.19
  2.7 0.1 clamp_convert_fusion
  2.8 0.6 %pad_maximum_fusion = bf16[32,4,128]{2,1,0:T(4,128)(2,1)} fusion(bf16[32,1,128]{2,1,0:T(2,128)(2,1)S(1)} %copy.19, bf16[32,3,128]{2,1,0:T(4,128)(2,1)S(1)} %clamp_convert_fusion), kind=kLoop, calls=%fused_computation.10 | loop fusion | flops 65536 | bytes 65536 | tf_op jit(solution)/shard_map/concatenate | solution.py:59
  3.5 7.3 %all-to-all-start = ((bf16[32,4,128]{2,1,0:T(4,128)(2,1)}), bf16[32,4,128]{2,1,0:T(4,128)(2,1)S(1)}, u32[]{:S(2)}, u32[]{:S(2)}) async-start(bf16[32,4,128]{2,1,0:T(4,128)(2,1)} %pad_maximum_fusion), calls=%async_computation | async-start | bytes 65536 | tf_op jit(solution)/shard_map/all_to_all | solution.py:60
  10.8 0.1 dynamic_slice.3
  10.9 7.2 %all-to-all-done = bf16[32,4,128]{2,1,0:T(4,128)(2,1)S(1)} async-done(((bf16[32,4,128]{2,1,0:T(4,128)(2,1)}), bf16[32,4,128]{2,1,0:T(4,128)(2,1)S(1)}, u32[]{:S(2)}, u32[]{:S(2)}) %all-to-all-start) | async-done | bytes 32800 | tf_op jit(solution)/shard_map/all_to_all | solution.py:60
  18.1 0.1 fusion.6
  18.2 0.1 fusion.10
  18.3 0.0 copy-start.1
  18.3 0.0 copy-start.2
  18.3 0.0 copy-start.3
  18.4 0.6 %copy-done.1 = f32[3,128]{1,0:T(4,128)S(1)} copy-done((f32[3,128]{1,0:T(4,128)S(1)}, f32[3,128]{1,0:T(4,128)}, u32[]{:S(2)}) %copy-start.1) | copy-done | bytes 1560
  19.0 0.0 copy-done.2
  19.0 0.0 copy-done.3
  19.0 0.7 %fusion.11 = (bf16[3,128]{1,0:T(4,128)(2,1)S(1)}, f32[3,128]{1,0:T(4,128)}, f32[3,128]{1,0:T(4,128)}, f32[3,128]{1,0:T(4,128)}) fusion(f32[3,128]{1,0:T(4,128)S(1)} %copy-done.1, f32[3,128]{1,0:T(4,128)S(1)} %convert_reduce_fusion, f32[3]{0:T(128)S(1)} %dynamic_slice.3, f32[3,128]{1,0:T(4,128)S(1)} %copy-done.2, f32[3,128]{1,0:T(4,128)S(1)} %copy-done.3), kind=kLoop, calls=%fused_computation.39 | loop fusion | flops 6528 | bytes 11532 | tf_op jit(solution)/shard_map/convert_element_type | solution.py:66
  19.7 9.0 %all_to_all.10 = bf16[32,4,128]{2,1,0:T(4,128)(2,1)S(1)} all-to-all(bf16[32,4,128]{2,1,0:T(4,128)(2,1)S(1)} %broadcast_in_dim.2), channel_id=1, replica_groups=mesh['dp'=8,'fsdp'=4] {'dp','fsdp'}, dimensions={0} | all-to-all | bytes 65536 | tf_op jit(solution)/shard_map/all_to_all | solution.py:68
  28.7 0.1 slice_add_fusion
  28.8 0.6 %reshape.36 = f32[96]{0:T(128)} reshape(f32[32,3]{1,0:T(8,128)S(1)} %slice_add_fusion) | data formatting | bytes 768 | tf_op jit(solution)/shard_map/reshape | solution.py:70
  29.4 0.6 %reshape.35 = bf16[96,128]{1,0:T(8,128)(2,1)} reshape(bf16[32,3,128]{2,1,0:T(4,128)(2,1)S(1)} %bitcast.9) | data formatting | bytes 49152 | tf_op jit(solution)/shard_map/reshape | solution.py:69
  (10 shorter events, 0.2 us)
Async XLA Ops:
  0.6 1.0 %copy-start = (f32[1,96,128]{2,1,0:T(8,128)S(1)}, f32[1,96,128]{2,1,0:T(8,128)}, u32[]{:S(2)}) copy-start(f32[1,96,128]{2,1,0:T(8,128)} %param.5) | copy-start | bytes 147460
  1.6 0.7 %copy-start.4 = (f32[96]{0:T(128)S(1)}, f32[96]{0:T(128)}, u32[]{:S(2)}) copy-start(f32[96]{0:T(128)} %param.6) | copy-start | bytes 1156
  3.5 14.6 %all-to-all-start = ((bf16[32,4,128]{2,1,0:T(4,128)(2,1)}), bf16[32,4,128]{2,1,0:T(4,128)(2,1)S(1)}, u32[]{:S(2)}, u32[]{:S(2)}) async-start(bf16[32,4,128]{2,1,0:T(4,128)(2,1)} %pad_maximum_fusion), calls=%async_computation | async-start | bytes 65536 | tf_op jit(solution)/shard_map/all_to_all | solution.py:60
  18.3 0.7 %copy-start.1 = (f32[3,128]{1,0:T(4,128)S(1)}, f32[3,128]{1,0:T(4,128)}, u32[]{:S(2)}) copy-start(f32[3,128]{1,0:T(4,128)} %param.7) | copy-start | bytes 4612
  18.3 0.7 %copy-start.2 = (f32[3,128]{1,0:T(4,128)S(1)}, f32[3,128]{1,0:T(4,128)}, u32[]{:S(2)}) copy-start(f32[3,128]{1,0:T(4,128)} %param.8) | copy-start | bytes 4612
  18.3 0.7 %copy-start.3 = (f32[3,128]{1,0:T(4,128)S(1)}, f32[3,128]{1,0:T(4,128)}, u32[]{:S(2)}) copy-start(f32[3,128]{1,0:T(4,128)} %param.9) | copy-start | bytes 4612
